TPU v7x, 256 devices: a whole 4x4x8 slice. The times are simulated.
256 devices in a mesh: grp: 4 (over y), dev: 64 (over z, x, core).
Axes of the slice: x: 4, y: 4, z: 8, core: 2. Of those that a mesh axis runs over, the one named last changes fastest.
Arguments:
- nz_user: int32 [32768, 128], P(('grp', 'dev')), may hold values from 0 to 65535
- nz_sub: int32 [32768, 128], P(('grp', 'dev')), may hold values from 0 to 16383
- nz_value: float32 [32768, 128], P(('grp', 'dev')), may hold values from -1 to 1
- tile_word: int32 [32768], P(('grp', 'dev')), may hold values from 0 to 16383, as said below
- word_owner: int32 [16384], replicated, may hold values from 0 to 16383, as said below
- user_factor: bfloat16 [64, 65536], P(None, 'dev'), may hold values from -6 to 6
- sub_factor: bfloat16 [64, 16384], P(None, 'dev'), may hold values from -6 to 6
Outputs:
- word_rows: float32 [64, 16384], P(None, ('grp', 'dev'))
Inputs may be any that keep to these rules, and one draw needn't show every extreme that they name: A permutation of the word indices: word w is summed into column word_owner[w] of word_rows. `tile_word`: tile i lies on device i // 128 (grp+dev order). On every device at most 2 tiles belong to words whose output column lies on any one other device, and on every device that bound is reached for some other device.
All inputs are finite; a program needn't handle non-finite values.
Results may differ from a plain program's by a relative error of at most 0.0003.
Values may be sent and summed in bfloat16 or wider, within the bound.
No kernel may reach another device: no remote copies, remote signals or barrier semaphores. Data moves between devices by JAX's collectives and lax.ppermute only.
A program may use at most 64 MiB of HBM per device.

v0:
```python
import jax
import jax.numpy as jnp
from jax import lax
from jax.sharding import PartitionSpec as P

CAP = 2


def cut_along(value, dim, peers):
    shape = value.shape
    pieces = value.reshape(*shape[:dim], peers, shape[dim] // peers, *shape[dim + 1 :])
    return jnp.moveaxis(pieces, dim, 0)


def joined_along(pieces, dim):
    pieces = jnp.moveaxis(pieces, 0, dim)
    shape = pieces.shape
    return pieces.reshape(*shape[:dim], shape[dim] * shape[dim + 1], *shape[dim + 2 :])


def exchange_both(value, axis, axes, splits, concats):
    sizes = [lax.axis_size(a) for a in axes]
    pieces = cut_along(value, splits[0], sizes[0])
    pieces = jnp.moveaxis(cut_along(pieces, splits[1] + 1, sizes[1]), 0, 1)
    inside = pieces.shape[2:]
    pieces = pieces.reshape(-1, *inside)
    pieces = lax.all_to_all(pieces, axis, split_axis=0, concat_axis=0, tiled=True)
    pieces = joined_along(pieces.reshape(*sizes, *inside), concats[0] + 1)
    return joined_along(pieces, concats[1])


def tile_sums(user_table, sub_table, nz_user, nz_sub, nz_value):
    tile_count, tile_width = nz_user.shape
    block_tiles = min(tile_count, 128)
    block_count = tile_count // block_tiles

    def one_block(block_args):
        users_block, subs_block, vals_block = block_args
        user_rows = jnp.take(user_table, users_block, axis=0).astype(jnp.float32)
        sub_rows = jnp.take(sub_table, subs_block, axis=0).astype(jnp.float32)
        return jnp.sum(user_rows * sub_rows * vals_block[:, :, None], axis=1)

    block_sums = lax.map(
        one_block,
        (
            nz_user.reshape(block_count, block_tiles, tile_width),
            nz_sub.reshape(block_count, block_tiles, tile_width),
            nz_value.reshape(block_count, block_tiles, tile_width),
        ),
    )
    return block_sums.reshape(tile_count, block_sums.shape[2])


def shards(nz_user, nz_sub, nz_value, tile_word, word_owner, user_factor, sub_factor):
    users_all, subs_all = (
        lax.all_gather(user_factor, "dev", axis=1, tiled=True),
        lax.all_gather(sub_factor, "dev", axis=1, tiled=True),
    )
    user_table = jnp.transpose(users_all)
    sub_table = jnp.transpose(subs_all)
    tile_rows = tile_sums(user_table, sub_table, nz_user, nz_sub, nz_value)
    tile_count, rank_width = tile_rows.shape
    grp_size = lax.axis_size("grp")
    dev_size = lax.axis_size("dev")
    devices_all = grp_size * dev_size
    words_total = word_owner.shape[0]
    words_local = words_total // devices_all
    out_rows = jnp.take(word_owner, tile_word)
    self_index = lax.axis_index("grp") * dev_size + lax.axis_index("dev")
    owner_dev = out_rows // words_local
    local_row = out_rows - owner_dev * words_local
    owned = owner_dev == self_index
    columns = jnp.arange(words_local, dtype=jnp.int32)
    own_table = (owned[:, None] & (local_row[:, None] == columns[None, :])).astype(jnp.float32)
    own_part = jnp.einsum("tr,tk->rk", tile_rows, own_table, precision=lax.Precision.HIGHEST)
    peer_ids = jnp.arange(devices_all, dtype=jnp.int32)
    outgoing = (jnp.logical_not(owned)[:, None] & (owner_dev[:, None] == peer_ids[None, :])).astype(
        jnp.float32
    )
    tile_ids = jnp.arange(tile_count, dtype=jnp.int32)
    earlier_table = (tile_ids[:, None] > tile_ids[None, :]).astype(jnp.float32)
    earlier = jnp.dot(
        earlier_table, outgoing, precision=lax.Precision.HIGHEST, preferred_element_type=jnp.float32
    )
    position = jnp.sum(earlier * outgoing, axis=1).astype(jnp.int32)
    send_slot = jnp.where(owned, devices_all * CAP, owner_dev * CAP + position)
    slot_ids = jnp.arange(devices_all * CAP, dtype=jnp.int32)
    slot_table = (send_slot[:, None] == slot_ids[None, :]).astype(jnp.float32)
    send_rows = jnp.einsum("ts,tr->sr", slot_table, tile_rows, precision=lax.Precision.HIGHEST)
    filled = jnp.sum(slot_table, axis=0)
    send_ids = (
        jnp.dot(
            local_row.astype(jnp.float32),
            slot_table,
            precision=lax.Precision.HIGHEST,
            preferred_element_type=jnp.float32,
        )
        + filled
        - 1.0
    )
    send_rows = send_rows.reshape(grp_size, dev_size, CAP * rank_width)
    send_ids = send_ids.reshape(grp_size, dev_size, CAP)
    got_rows, got_ids = (
        exchange_both(send_rows, ("dev", "grp"), ("dev", "grp"), (1, 0), (1, 0)),
        exchange_both(send_ids, ("dev", "grp"), ("dev", "grp"), (1, 0), (1, 0)),
    )
    got_rows = got_rows.reshape(devices_all * CAP, rank_width)
    got_ids = got_ids.reshape(devices_all * CAP).astype(jnp.int32)
    got_table = (got_ids[:, None] == columns[None, :]).astype(jnp.float32)
    far_part = jnp.einsum("sr,sk->rk", got_rows, got_table, precision=lax.Precision.HIGHEST)
    return own_part + far_part


def solution(mesh):
    return jax.shard_map(
        shards,
        mesh=mesh,
        in_specs=(
            P(("grp", "dev"), None),
            P(("grp", "dev"), None),
            P(("grp", "dev"), None),
            P(("grp", "dev")),
            P(),
            P(None, "dev"),
            P(None, "dev"),
        ),
        out_specs=P(None, ("grp", "dev")),
        check_vma=False,
    )
```

profile of v0, /device:TPU:1, one launch (start us, length us, event | category | flops | bytes accessed | tf_op | source)
XLA Modules:
  0.0 297.3 jit_solution(12197286190946821888)
XLA Ops:
  6.5 0.0 copy-start
  6.5 0.0 all-gather.5.cloned.1.call-start
  6.5 1.5 copy.45
  8.1 0.0 all-gather.5.cloned.1.call-update
  8.1 0.0 all-gather.3.cloned.1.call-start
  8.1 1.8 copy.44
  9.9 0.0 all-gather.3.cloned.1.call-update
  9.9 0.7 compare_select_fusion.2
  10.6 0.0 copy-done
  10.6 1.1 gather_fusion.2
  11.8 0.7 fusion.17
  12.4 0.3 fusion
  12.8 0.7 add_select_fusion
  13.4 0.1 convert_reduce_fusion
  13.6 0.3 fusion.1
  13.8 0.1 reshape_reshape.14
  14.0 0.7 copy.55
  14.7 15.6 %all-to-all-start.1 = ((f32[256,1,1,2]{3,2,1,0:T(1,128)}), f32[256,1,1,2]{3,2,1,0:T(1,128)S(1)}, u32[]{:S(2)}, u32[]{:S(2)}) async-start(f32[256,1,1,2]{3,2,1,0:T(1,128)} %bitcast.14), calls=%async_computation.1 | async-start | bytes 262144 | tf_op jit(solution)/shard_map/all_to_all | solution.py:27
  30.4 0.9 compare_and_fusion
  31.3 0.9 bitcast_clamp_fusion.1
  32.1 0.9 bitcast_clamp_fusion
  33.0 60.6 %all-gather.5.cloned.1.call-done = bf16[64,16384]{0,1:T(8,128)(2,1)} async-done(((bf16[64,256]{0,1:T(8,128)(2,1)}), bf16[64,16384]{0,1:T(8,128)(2,1)}) %all-gather.5.cloned.1.call-update) | async-done | bytes 2097168 | tf_op jit(solution)/shard_map/all_gather | solution.py:57
  93.6 58.1 %gather_fusion.1 = bf16[16384,64]{1,0:T(8,128)(2,1)} fusion(bf16[16384,64]{1,0:T(8,128)(2,1)} %bitcast.38, s32[16384]{0:T(1024)S(1)} %bitcast_clamp_fusion), kind=kCustom, calls=%fused_computation.1 | custom fusion | bytes 4259840 | tf_op jit(solution)/shard_map/while/body/eval_jaxpr/jit(_take)/gather | solution.py:40
  151.8 41.1 %all-gather.3.cloned.1.call-done = bf16[64,65536]{0,1:T(8,128)(2,1)} async-done(((bf16[64,1024]{0,1:T(8,128)(2,1)}), bf16[64,65536]{0,1:T(8,128)(2,1)}) %all-gather.3.cloned.1.call-update) | async-done | bytes 8388624 | tf_op jit(solution)/shard_map/all_gather | solution.py:56
  192.8 0.0 copy-start.1
  192.8 63.3 %gather_fusion = bf16[16384,64]{1,0:T(8,128)(2,1)} fusion(bf16[65536,64]{1,0:T(8,128)(2,1)} %bitcast.39, s32[16384]{0:T(1024)S(1)} %bitcast_clamp_fusion.1), kind=kCustom, calls=%fused_computation | custom fusion | bytes 4259840 | tf_op jit(solution)/shard_map/while/body/eval_jaxpr/jit(_take)/gather | solution.py:39
  256.2 0.0 copy-done.1
  256.2 10.6 %multiply_reduce_fusion = f32[128,64]{1,0:T(8,128)S(1)} fusion(f32[128,128]{1,0:T(8,128)S(1)} %copy-done.1, pred[128,128]{1,0:T(8,128)(4,1)S(1)} %get-tuple-element.30, pred[128,128]{1,0:T(8,128)(4,1)S(1)} %get-tuple-element.32, bf16[16384,64]{1,0:T(8,128)(2,1)} %gather_fusion.1, bf16[16384,64]{1,0:T(8,128)(2,1)} %gather_fusion), kind=kLoop, calls=%fused_computation.3 | loop fusion | flops 7331840 | bytes 4325376 | tf_op jit(solution)/shard_map/while/body/eval_jaxpr/reduce_sum | solution.py:41
  266.8 0.5 fusion.2
  267.2 0.1 reshape_reshape.12
  267.3 0.7 copy.47
  268.1 0.0 all-to-all-done.1
  268.1 8.5 %all-to-all-start = ((f32[256,1,1,128]{3,2,1,0:T(1,128)}), f32[256,1,1,128]{3,2,1,0:T(1,128)S(1)}, u32[]{:S(2)}, u32[]{:S(2)}) async-start(f32[256,1,1,128]{3,2,1,0:T(1,128)} %bitcast.8), calls=%async_computation | async-start | bytes 262144 | tf_op jit(solution)/shard_map/all_to_all | solution.py:27
  276.6 0.1 copy.52
  276.6 0.1 convert_element_type.45
  276.8 0.6 copy.53
  277.3 0.2 convert_element_type.47
  277.5 0.3 fusion.11
  277.8 11.5 %all-to-all-done = f32[256,1,1,128]{3,2,1,0:T(1,128)S(1)} async-done(((f32[256,1,1,128]{3,2,1,0:T(1,128)}), f32[256,1,1,128]{3,2,1,0:T(1,128)S(1)}, u32[]{:S(2)}, u32[]{:S(2)}) %all-to-all-start) | async-done | bytes 131104 | tf_op jit(solution)/shard_map/all_to_all | solution.py:27
  289.3 0.1 reshape_reshape_reshape.4
  289.4 1.1 convolution_add_fusion
  (4 shorter events, 0.0 us)
Async XLA Ops:
  6.5 4.1 %copy-start = (s32[16384]{0:T(1024)S(1)}, s32[16384]{0:T(1024)}, u32[]{:S(2)}) copy-start(s32[16384]{0:T(1024)} %param.11) | copy-start | bytes 196612
  6.5 87.1 %all-gather.5.cloned.1.call-start = ((), (), s32[]{:S(2)}) async-start(), calls=%async_computation.3 | async-start | bytes 4259840 | tf_op jit(solution)/shard_map/all_gather | solution.py:57
  8.1 184.8 %all-gather.3.cloned.1.call-start = ((), (), s32[]{:S(2)}) async-start(), calls=%async_computation.2 | async-start | bytes 17039360 | tf_op jit(solution)/shard_map/all_gather | solution.py:56
  14.7 253.4 %all-to-all-start.1 = ((f32[256,1,1,2]{3,2,1,0:T(1,128)}), f32[256,1,1,2]{3,2,1,0:T(1,128)S(1)}, u32[]{:S(2)}, u32[]{:S(2)}) async-start(f32[256,1,1,2]{3,2,1,0:T(1,128)} %bitcast.14), calls=%async_computation.1 | async-start | bytes 262144 | tf_op jit(solution)/shard_map/all_to_all | solution.py:27
  192.8 63.3 %copy-start.1 = (f32[128,128]{1,0:T(8,128)S(1)}, f32[128,128]{1,0:T(8,128)}, u32[]{:S(2)}) copy-start(f32[128,128]{1,0:T(8,128)} %param.9) | copy-start | bytes 196612
  268.1 21.2 %all-to-all-start = ((f32[256,1,1,128]{3,2,1,0:T(1,128)}), f32[256,1,1,128]{3,2,1,0:T(1,128)S(1)}, u32[]{:S(2)}, u32[]{:S(2)}) async-start(f32[256,1,1,128]{3,2,1,0:T(1,128)} %bitcast.8), calls=%async_computation | async-start | bytes 262144 | tf_op jit(solution)/shard_map/all_to_all | solution.py:27
Sparse Core Ops, SparseCore 0:
  10.1 83.5 all-gather.4
  96.4 96.3 all-gather.2
where the time goes:
time: 298 us; the launch traced here: 297 us
  local copies, waits for them, and re-layouts  129 us (43%)
  waiting for transfers between devices  113 us (38%)
  starting transfers between devices  24.2 us (8%)
  other arithmetic  15.4 us (5%)
  between operations  13.5 us (5%)
    gather x1, local copies, waits for them, and re-layouts, one_block(): user_rows = jnp.take(user_table, users_block, axis=0).astype(jnp.float32)  63.3 us
    all_gather x1, waiting for transfers between devices, shards(): lax.all_gather(sub_factor, 'dev', axis=1, tiled=True)  60.6 us
    gather x1, local copies, waits for them, and re-layouts, one_block(): sub_rows = jnp.take(sub_table, subs_block, axis=0).astype(jnp.float32)  58.1 us
    all_gather x1, waiting for transfers between devices, shards(): lax.all_gather(user_factor, 'dev', axis=1, tiled=True)  41.1 us
    all_to_all x2, starting transfers between devices, exchange_both(): lax.all_to_all(pieces, axis, split_axis=0, concat_axis=0, tiled=True)  24.1 us
    all_to_all x2, waiting for transfers between devices, exchange_both(): lax.all_to_all(pieces, axis, split_axis=0, concat_axis=0, tiled=True)  11.5 us
    reduce_sum x1, other arithmetic, one_block(): return jnp.sum(user_rows * sub_rows * vals_block[:, :, None], axis=1)  10.6 us
  transfers between devices with their start and end apart: 4, of which 3 were waited for; matrix products, arithmetic and copies ran while one was open for 48% of the time, Pallas kernels for 0%

commit v1 on v0

--- a/solution.py
+++ b/solution.py
@@ -53,7 +53,9 @@
 
 def shards(nz_user, nz_sub, nz_value, tile_word, word_owner, user_factor, sub_factor):
     users_all, subs_all = (
-        lax.all_gather(user_factor, "dev", axis=1, tiled=True),
+        jnp.concatenate(
+            lax.all_to_all(jnp.stack([user_factor] * lax.axis_size("dev")), "dev", 0, 0), axis=1
+        ),
         lax.all_gather(sub_factor, "dev", axis=1, tiled=True),
     )
     user_table = jnp.transpose(users_all)

time: 298 us -> 358 us (1.20)
  waiting for transfers between devices: 113 us -> 145 us
  local copies, waits for them, and re-layouts: 129 us -> 146 us
  starting transfers between devices: 24.2 us -> 39.6 us
  other arithmetic: 15.4 us -> 10.8 us
    all_gather x1, waiting for transfers between devices: 60.6 us -> 112 us  [shards(): lax.all_gather(sub_factor, 'dev', axis=1, tiled=True)]
    all_gather x1 -> x0, waiting for transfers between devices: 41.1 us -> none  [shards(): lax.all_gather(user_factor, 'dev', axis=1, tiled=True)]
    all_to_all x0 -> x1, waiting for transfers between devices: none -> 21.1 us  [shards(): lax.all_to_all(jnp.stack([user_factor] * lax.axis_size('dev')), 'dev', 0, 0)]
    reshape x0 -> x1, local copies, waits for them, and re-layouts: none -> 15.5 us  [shards(): jnp.concatenate(lax.all_to_all(jnp.stack([user_factor] * lax.axis_size('d...]
    all_to_all x0 -> x1, starting transfers between devices: none -> 13.3 us  [shards(): lax.all_to_all(jnp.stack([user_factor] * lax.axis_size('dev')), 'dev', 0, 0)]
    another operation x0 -> x1, local copies, waits for them, and re-layouts: none -> 5.23 us  [shards(): jnp.stack([user_factor] * lax.axis_size('dev'))]
  transfers between devices with their start and end apart: 4 -> 4, of which waited for: 3 -> 3; matrix products, arithmetic and copies ran while one was open for 48% -> 43% of each run, Pallas kernels for 0% -> 0%
where the time goes in v1:
time: 358 us; the launch traced here: 357 us
  local copies, waits for them, and re-layouts  146 us (41%)
  waiting for transfers between devices  145 us (41%)
  starting transfers between devices  39.6 us (11%)
  between operations  13.6 us (4%)
  other arithmetic  10.8 us (3%)
    all_gather x1, waiting for transfers between devices, shards(): lax.all_gather(sub_factor, 'dev', axis=1, tiled=True)  112 us
    gather x1, local copies, waits for them, and re-layouts, one_block(): user_rows = jnp.take(user_table, users_block, axis=0).astype(jnp.float32)  62.9 us
    gather x1, local copies, waits for them, and re-layouts, one_block(): sub_rows = jnp.take(sub_table, subs_block, axis=0).astype(jnp.float32)  57.7 us
    all_to_all x2, starting transfers between devices, exchange_both(): lax.all_to_all(pieces, axis, split_axis=0, concat_axis=0, tiled=True)  26.3 us
    all_to_all x1, waiting for transfers between devices, shards(): lax.all_to_all(jnp.stack([user_factor] * lax.axis_size('dev')), 'dev', 0, 0)  21.1 us
    reshape x1, local copies, waits for them, and re-layouts, shards(): jnp.concatenate(lax.all_to_all(jnp.stack([user_factor] * lax.axis_size('d...  15.5 us
    all_to_all x1, starting transfers between devices, shards(): lax.all_to_all(jnp.stack([user_factor] * lax.axis_size('dev')), 'dev', 0, 0)  13.3 us
    all_to_all x2, waiting for transfers between devices, exchange_both(): lax.all_to_all(pieces, axis, split_axis=0, concat_axis=0, tiled=True)  11.5 us
  transfers between devices with their start and end apart: 4, of which 3 were waited for; matrix products, arithmetic and copies ran while one was open for 43% of the time, Pallas kernels for 0%

profile of v1, /device:TPU:1, one launch (start us, length us, event | category | flops | bytes accessed | tf_op | source)
XLA Modules:
  0.0 357.3 jit_solution(3798404651440714828)
XLA Ops:
  6.5 0.0 copy-start
  6.5 5.2 %stack.2 = bf16[64,64,1024]{2,1,0:T(8,128)(2,1)} broadcast(bf16[64,1024]{1,0:T(8,128)(2,1)} %param.12), dimensions={1,2} | broadcast | bytes 8519680 | tf_op jit(solution)/shard_map/stack | solution.py:57
  11.8 0.0 copy-start.4
  11.8 0.0 copy-start.5
  11.8 0.0 copy-start.1
  11.8 0.0 copy-start.2
  11.8 13.3 %all-to-all-start = ((bf16[64,64,1024]{2,1,0:T(8,128)(2,1)}), bf16[64,64,1024]{2,1,0:T(8,128)(2,1)}, u32[]{:S(2)}, u32[]{:S(2)}) async-start(bf16[64,64,1024]{2,1,0:T(8,128)(2,1)} %stack.2), calls=%async_computation | async-start | bytes 16777216 | tf_op jit(solution)/shard_map/all_to_all | solution.py:57
  25.1 0.0 all-gather.2.cloned.1.call-start
  25.1 0.0 copy-done.4
  25.2 0.7 copy.45
  25.9 0.0 all-gather.2.cloned.1.call-update
  25.9 0.0 copy-done.5
  25.9 0.0 copy-done
  26.0 1.1 gather_fusion.2
  27.1 0.3 fusion
  27.5 0.1 convert_reduce_fusion
  27.6 0.3 fusion.1
  27.9 0.1 reshape_reshape.14
  28.0 0.7 copy.55
  28.8 0.0 copy-done.1
  28.8 0.0 copy-done.2
  28.9 112.2 %all-gather.2.cloned.1.call-done = bf16[64,16384]{0,1:T(8,128)(2,1)} async-done(((bf16[64,256]{0,1:T(8,128)(2,1)}), bf16[64,16384]{0,1:T(8,128)(2,1)}) %all-gather.2.cloned.1.call-update) | async-done | bytes 2097168 | tf_op jit(solution)/shard_map/all_gather | solution.py:59
  141.1 57.7 %gather_fusion.1 = bf16[16384,64]{1,0:T(8,128)(2,1)} fusion(bf16[16384,64]{1,0:T(8,128)(2,1)} %bitcast.41, s32[16384]{0:T(1024)S(1)} %bitcast_clamp_fusion), kind=kCustom, calls=%fused_computation.1 | custom fusion | bytes 4259840 | tf_op jit(solution)/shard_map/while/body/eval_jaxpr/jit(_take)/gather | solution.py:40
  198.7 21.1 %all-to-all-done = bf16[64,64,1024]{2,1,0:T(8,128)(2,1)} async-done(((bf16[64,64,1024]{2,1,0:T(8,128)(2,1)}), bf16[64,64,1024]{2,1,0:T(8,128)(2,1)}, u32[]{:S(2)}, u32[]{:S(2)}) %all-to-all-start) | async-done | bytes 8388640 | tf_op jit(solution)/shard_map/all_to_all | solution.py:57
  219.9 12.6 %all-to-all-start.2 = ((f32[256,1,1,2]{3,2,1,0:T(1,128)}), f32[256,1,1,2]{3,2,1,0:T(1,128)S(1)}, u32[]{:S(2)}, u32[]{:S(2)}) async-start(f32[256,1,1,2]{3,2,1,0:T(1,128)} %bitcast.16), calls=%async_computation.2 | async-start | bytes 262144 | tf_op jit(solution)/shard_map/all_to_all | solution.py:27
  232.4 15.5 %copy.44 = bf16[64,64,1024]{0,2,1:T(8,128)(2,1)} copy(bf16[64,64,1024]{2,0,1:T(8,128)(2,1)} %bitcast) | data formatting | bytes 16777216 | tf_op jit(solution)/shard_map/reshape | solution.py:56
  248.0 0.0 copy-start.3
  248.0 62.9 %gather_fusion = bf16[16384,64]{1,0:T(8,128)(2,1)} fusion(bf16[65536,64]{1,0:T(8,128)(2,1)} %bitcast.42, s32[16384]{0:T(1024)S(1)} %bitcast_clamp_fusion.1), kind=kCustom, calls=%fused_computation | custom fusion | bytes 4259840 | tf_op jit(solution)/shard_map/while/body/eval_jaxpr/jit(_take)/gather | solution.py:39
  310.9 0.0 copy-done.3
  310.9 10.6 %multiply_reduce_fusion = f32[128,64]{1,0:T(8,128)S(1)} fusion(f32[128,128]{1,0:T(8,128)S(1)} %copy-done.3, pred[128,128]{1,0:T(8,128)(4,1)S(1)} %get-tuple-element.30, pred[128,128]{1,0:T(8,128)(4,1)S(1)} %get-tuple-element.32, bf16[16384,64]{1,0:T(8,128)(2,1)} %gather_fusion.1, bf16[16384,64]{1,0:T(8,128)(2,1)} %gather_fusion), kind=kLoop, calls=%fused_computation.3 | loop fusion | flops 7331840 | bytes 4325376 | tf_op jit(solution)/shard_map/while/body/eval_jaxpr/reduce_sum | solution.py:41
  321.5 0.5 fusion.2
  321.9 0.1 reshape_reshape.12
  322.0 0.7 copy.47
  322.8 0.0 all-to-all-done.2
  322.8 13.7 %all-to-all-start.1 = ((f32[256,1,1,128]{3,2,1,0:T(1,128)}), f32[256,1,1,128]{3,2,1,0:T(1,128)S(1)}, u32[]{:S(2)}, u32[]{:S(2)}) async-start(f32[256,1,1,128]{3,2,1,0:T(1,128)} %bitcast.10), calls=%async_computation.1 | async-start | bytes 262144 | tf_op jit(solution)/shard_map/all_to_all | solution.py:27
  336.5 0.1 copy.52
  336.6 0.1 convert_element_type.45
  336.7 0.6 copy.53
  337.3 0.2 convert_element_type.47
  337.4 0.3 fusion.11
  337.7 11.5 %all-to-all-done.1 = f32[256,1,1,128]{3,2,1,0:T(1,128)S(1)} async-done(((f32[256,1,1,128]{3,2,1,0:T(1,128)}), f32[256,1,1,128]{3,2,1,0:T(1,128)S(1)}, u32[]{:S(2)}, u32[]{:S(2)}) %all-to-all-start.1) | async-done | bytes 131104 | tf_op jit(solution)/shard_map/all_to_all | solution.py:27
  349.2 0.1 reshape_reshape_reshape.4
  349.3 1.1 convolution_add_fusion
  (10 shorter events, 0.1 us)
Async XLA Ops:
  6.5 19.4 %copy-start = (s32[16384]{0:T(1024)S(1)}, s32[16384]{0:T(1024)}, u32[]{:S(2)}) copy-start(s32[16384]{0:T(1024)} %param.11) | copy-start | bytes 196612
  11.8 13.4 %copy-start.4 = (bf16[64,256]{1,0:T(8,128)(2,1)S(1)}, bf16[64,256]{1,0:T(8,128)(2,1)}, u32[]{:S(2)}) copy-start(bf16[64,256]{1,0:T(8,128)(2,1)} %param.13) | copy-start | bytes 98308
  11.8 14.1 %copy-start.5 = (s32[128]{0:T(128)S(1)}, s32[128]{0:T(128)}, u32[]{:S(2)}) copy-start(s32[128]{0:T(128)} %param.10) | copy-start | bytes 1540
  11.8 17.0 %copy-start.1 = (s32[128,128]{1,0:T(8,128)S(1)}, s32[128,128]{1,0:T(8,128)}, u32[]{:S(2)}) copy-start(s32[128,128]{1,0:T(8,128)} %param.7) | copy-start | bytes 196612
  11.8 17.0 %copy-start.2 = (s32[128,128]{1,0:T(8,128)S(1)}, s32[128,128]{1,0:T(8,128)}, u32[]{:S(2)}) copy-start(s32[128,128]{1,0:T(8,128)} %param.8) | copy-start | bytes 196612
  11.8 208.1 %all-to-all-start = ((bf16[64,64,1024]{2,1,0:T(8,128)(2,1)}), bf16[64,64,1024]{2,1,0:T(8,128)(2,1)}, u32[]{:S(2)}, u32[]{:S(2)}) async-start(bf16[64,64,1024]{2,1,0:T(8,128)(2,1)} %stack.2), calls=%async_computation | async-start | bytes 16777216 | tf_op jit(solution)/shard_map/all_to_all | solution.py:57
  25.1 116.0 %all-gather.2.cloned.1.call-start = ((), (), s32[]{:S(2)}) async-start(), calls=%async_computation.3 | async-start | bytes 4259840 | tf_op jit(solution)/shard_map/all_gather | solution.py:59
  219.9 102.9 %all-to-all-start.2 = ((f32[256,1,1,2]{3,2,1,0:T(1,128)}), f32[256,1,1,2]{3,2,1,0:T(1,128)S(1)}, u32[]{:S(2)}, u32[]{:S(2)}) async-start(f32[256,1,1,2]{3,2,1,0:T(1,128)} %bitcast.16), calls=%async_computation.2 | async-start | bytes 262144 | tf_op jit(solution)/shard_map/all_to_all | solution.py:27
  248.0 62.9 %copy-start.3 = (f32[128,128]{1,0:T(8,128)S(1)}, f32[128,128]{1,0:T(8,128)}, u32[]{:S(2)}) copy-start(f32[128,128]{1,0:T(8,128)} %param.9) | copy-start | bytes 196612
  322.8 26.4 %all-to-all-start.1 = ((f32[256,1,1,128]{3,2,1,0:T(1,128)}), f32[256,1,1,128]{3,2,1,0:T(1,128)S(1)}, u32[]{:S(2)}, u32[]{:S(2)}) async-start(f32[256,1,1,128]{3,2,1,0:T(1,128)} %bitcast.10), calls=%async_computation.1 | async-start | bytes 262144 | tf_op jit(solution)/shard_map/all_to_all | solution.py:27
Sparse Core Ops, SparseCore 0:
  28.7 112.3 all-gather.1
